TPU v7x, 16 devices: a whole 2x2x2 slice. The times are simulated.
16 devices in a mesh: rep: 1, dp: 16 (over x, y, z, core).
Axes of the slice: x: 2, y: 2, z: 2, core: 2. Of those that a mesh axis runs over, the one named last changes fastest.
Arguments:
- g_w_gate: bfloat16 [16, 2, 896, 2560], P(('rep', 'dp'))
- g_w_up: bfloat16 [16, 2, 896, 2560], P(('rep', 'dp'))
- g_w_down: bfloat16 [16, 2, 2560, 896], P(('rep', 'dp'))
- w_gate: bfloat16 [2, 896, 2560], replicated
- w_up: bfloat16 [2, 896, 2560], replicated
- w_down: bfloat16 [2, 2560, 896], replicated
- m_w_gate: float32 [2, 896, 2560], P(None, 'dp')
- m_w_up: float32 [2, 896, 2560], P(None, 'dp')
- m_w_down: float32 [2, 2560, 896], P(None, 'dp')
- v_w_gate: float32 [2, 896, 2560], P(None, 'dp')
- v_w_up: float32 [2, 896, 2560], P(None, 'dp')
- v_w_down: float32 [2, 2560, 896], P(None, 'dp')
Outputs:
- output 1: bfloat16 [2, 896, 2560], P('rep')
- output 2: bfloat16 [2, 896, 2560], P('rep')
- output 3: bfloat16 [2, 2560, 896], P('rep')
- output 4: float32 [2, 896, 2560], P('rep', 'dp')
- output 5: float32 [2, 896, 2560], P('rep', 'dp')
- output 6: float32 [2, 2560, 896], P('rep', 'dp')
- output 7: float32 [2, 896, 2560], P('rep', 'dp')
- output 8: float32 [2, 896, 2560], P('rep', 'dp')
- output 9: float32 [2, 2560, 896], P('rep', 'dp')
All inputs are finite; a program needn't handle non-finite values.
Results may differ from a plain program's by a relative error of at most 0.022.
Values are sent between devices in bfloat16 or wider.
A program may use at most 2 GiB of HBM per device.

v0:
```python
import jax
import jax.numpy as jnp
from jax import lax
from jax.sharding import PartitionSpec as P


def adamw(w, m, v, g):
    m = 0.9 * m + 0.1 * g
    v = 0.95 * v + 0.05 * g * g
    step = m * lax.rsqrt(v + 1e-8) + 0.1 * w
    return (w - 0.02 * step).astype(jnp.bfloat16), m, v


def solution(mesh):
    def step(*arrays):
        terms, weights, m, v = (arrays[i : i + 3] for i in (0, 3, 6, 9))
        gradients = [lax.psum_scatter(t[0], "dp", scatter_dimension=1, tiled=True).astype(jnp.float32) for t in terms]
        me = lax.axis_index("dp")
        own = [lax.dynamic_slice_in_dim(w, me * one.shape[1], one.shape[1], 1).astype(jnp.float32) for w, one in zip(weights, m, strict=True)]
        new = [adamw(w, m, v, g) for w, m, v, g in zip(own, m, v, gradients, strict=True)]
        whole = [lax.all_gather(one[0], "dp", axis=1, tiled=True) for one in new]
        return (*whole, *(one[1] for one in new), *(one[2] for one in new))

    all_of, cut = P(None, None, None), P(None, "dp", None)
    return jax.shard_map(
        step,
        mesh=mesh,
        in_specs=(P(("rep", "dp"), None, None, None),) * 3 + (all_of,) * 3 + (cut,) * 6,
        out_specs=(P("rep", None, None),) * 3 + (P("rep", "dp", None),) * 6,
        check_vma=False,
    )
```

profile of v0, /device:TPU:0, one launch (start us, length us, event | category | flops | bytes accessed | tf_op | source)
XLA Modules:
  0.0 514.3 jit_solution(3536751875570039160)
XLA Ops:
  7.2 0.0 reduce-scatter.8.cloned.1.call-start
  7.2 0.7 reduce-scatter.8.cloned.1.call-update
  7.9 0.0 reduce-scatter.10.cloned.1.call-start
  8.0 39.1 %copy.21 = bf16[2,896,2560]{2,0,1:T(2,128)(2,1)} copy(bf16[2,896,2560]{2,1,0:T(8,128)(2,1)} %bitcast.15) | data formatting | bytes 18350080
  47.1 9.6 %copy.25 = bf16[112,8,2,2560]{3,1,2,0:T(8,128)(2,1)} copy(bf16[112,8,2,2560]{3,2,1,0:T(2,128)(2,1)} %bitcast.13) | data formatting | bytes 18350080
  56.7 0.0 reduce-scatter.10.cloned.1.call-update
  56.7 0.0 reduce-scatter.12.cloned.1.call-start
  56.7 39.1 %copy.23 = bf16[2,896,2560]{2,0,1:T(2,128)(2,1)} copy(bf16[2,896,2560]{2,1,0:T(8,128)(2,1)} %bitcast.16) | data formatting | bytes 18350080
  95.8 9.6 %copy.26 = bf16[112,8,2,2560]{3,1,2,0:T(8,128)(2,1)} copy(bf16[112,8,2,2560]{3,2,1,0:T(2,128)(2,1)} %bitcast.14) | data formatting | bytes 18350080
  105.4 0.0 reduce-scatter.12.cloned.1.call-update
  105.5 0.0 all-gather.8.cloned.1.call-start
  105.5 6.7 %reduce-scatter.8.cloned.1.call-done = bf16[2,160,896]{2,1,0:T(8,128)(2,1)} async-done(((bf16[2,2560,896]{2,1,0:T(8,128)(2,1)}), bf16[2,160,896]{2,1,0:T(8,128)(2,1)}) %reduce-scatter.8.cloned.1.call-update) | async-done | bytes 573456 | tf_op jit(solution)/shard_map/reduce_scatter | solution.py:17
  112.2 0.0 copy-done
  112.2 3.2 fusion.10
  115.4 0.0 all-gather.8.cloned.1.call-update
  115.4 0.0 all-gather.4.cloned.1.call-start
  115.5 100.7 %reduce-scatter.10.cloned.1.call-done = bf16[56,5120]{1,0:T(8,128)(2,1)} async-done(((bf16[896,5120]{1,0:T(8,128)(2,1)}), bf16[56,5120]{1,0:T(8,128)(2,1)}) %reduce-scatter.10.cloned.1.call-update) | async-done | bytes 573456
  216.1 1.5 reshape.19
  217.6 2.9 fusion.2
  220.6 0.0 all-gather.4.cloned.1.call-update
  220.6 0.2 all-gather.6.cloned.1.call-start
  220.9 99.5 %reduce-scatter.12.cloned.1.call-done = bf16[56,5120]{1,0:T(8,128)(2,1)} async-done(((bf16[896,5120]{1,0:T(8,128)(2,1)}), bf16[56,5120]{1,0:T(8,128)(2,1)}) %reduce-scatter.12.cloned.1.call-update) | async-done | bytes 573456
  320.4 1.5 reshape.21
  321.9 0.0 copy-done.4
  321.9 3.3 fusion.6
  325.2 0.0 all-gather.6.cloned.1.call-update
  325.2 50.4 %all-gather.8.cloned.1.call-done = bf16[2,2560,896]{2,1,0:T(8,128)(2,1)} async-done(((bf16[2,160,896]{2,1,0:T(8,128)(2,1)}), bf16[2,2560,896]{2,1,0:T(8,128)(2,1)}) %all-gather.8.cloned.1.call-update) | async-done | bytes 9175056 | tf_op jit(solution)/shard_map/all_gather | solution.py:21
  375.7 54.0 %all-gather.4.cloned.1.call-done = bf16[2,896,2560]{2,1,0:T(8,128)(2,1)} async-done(((bf16[2,56,2560]{2,1,0:T(8,128)(2,1)}), bf16[2,896,2560]{2,1,0:T(8,128)(2,1)}) %all-gather.4.cloned.1.call-update) | async-done | bytes 9175056 | tf_op jit(solution)/shard_map/all_gather | solution.py:21
  429.7 54.1 %all-gather.6.cloned.1.call-done = bf16[2,896,2560]{2,1,0:T(8,128)(2,1)} async-done(((bf16[2,56,2560]{2,1,0:T(8,128)(2,1)}), bf16[2,896,2560]{2,1,0:T(8,128)(2,1)}) %all-gather.6.cloned.1.call-update) | async-done | bytes 9175056 | tf_op jit(solution)/shard_map/all_gather | solution.py:21
  483.8 7.8 %copy.38 = bf16[2,896,2560]{2,1,0:T(8,128)(2,1)} copy(bf16[2,896,2560]{2,1,0:T(8,128)(2,1)} %all-gather.4.cloned.1.call-done) | data formatting | bytes 18350080
  491.6 7.8 %copy.39 = bf16[2,896,2560]{2,1,0:T(8,128)(2,1)} copy(bf16[2,896,2560]{2,1,0:T(8,128)(2,1)} %all-gather.6.cloned.1.call-done) | data formatting | bytes 18350080
  499.5 8.0 %copy.40 = bf16[2,2560,896]{2,1,0:T(8,128)(2,1)} copy(bf16[2,2560,896]{2,1,0:T(8,128)(2,1)} %all-gather.8.cloned.1.call-done) | data formatting | bytes 18350080
  (8 shorter events, 0.0 us)
Async XLA Ops:
  7.2 105.0 %reduce-scatter.8.cloned.1.call-start = ((), (), s32[]{:S(2)}) async-start(), calls=%async_computation.5 | async-start | bytes 9748480 | tf_op jit(solution)/shard_map/reduce_scatter | solution.py:17
  7.9 208.2 %reduce-scatter.10.cloned.1.call-start = ((), (), s32[]{:S(2)}) async-start(), calls=%async_computation.7 | async-start | bytes 9748480
  56.7 263.7 %reduce-scatter.12.cloned.1.call-start = ((), (), s32[]{:S(2)}) async-start(), calls=%async_computation.8 | async-start | bytes 9748480
  105.4 6.8 %copy-start = (f32[2,160,896]{2,1,0:T(8,128)S(1)}, f32[2,160,896]{2,1,0:T(8,128)}, u32[]{:S(2)}) copy-start(f32[2,160,896]{2,1,0:T(8,128)} %param.23) | copy-start | bytes 3440644
  105.4 6.8 %copy-start.1 = (f32[2,160,896]{2,1,0:T(8,128)S(1)}, f32[2,160,896]{2,1,0:T(8,128)}, u32[]{:S(2)}) copy-start(f32[2,160,896]{2,1,0:T(8,128)} %param.20) | copy-start | bytes 3440644
  105.5 270.2 %all-gather.8.cloned.1.call-start = ((), (), s32[]{:S(2)}) async-start(), calls=%async_computation.6 | async-start | bytes 9748480 | tf_op jit(solution)/shard_map/all_gather | solution.py:21
  112.2 105.4 %copy-start.3 = (f32[2,56,2560]{2,1,0:T(8,128)S(1)}, f32[2,56,2560]{2,1,0:T(8,128)}, u32[]{:S(2)}) copy-start(f32[2,56,2560]{2,1,0:T(8,128)} %param.18) | copy-start | bytes 3440644
  115.4 102.3 %copy-start.2 = (f32[2,56,2560]{2,1,0:T(8,128)S(1)}, f32[2,56,2560]{2,1,0:T(8,128)}, u32[]{:S(2)}) copy-start(f32[2,56,2560]{2,1,0:T(8,128)} %param.21) | copy-start | bytes 3440644
  115.4 314.3 %all-gather.4.cloned.1.call-start = ((), (), s32[]{:S(2)}) async-start(), calls=%async_computation.3 | async-start | bytes 9748480 | tf_op jit(solution)/shard_map/all_gather | solution.py:21
  220.6 101.3 %copy-start.4 = (f32[2,56,2560]{2,1,0:T(8,128)S(1)}, f32[2,56,2560]{2,1,0:T(8,128)}, u32[]{:S(2)}) copy-start(f32[2,56,2560]{2,1,0:T(8,128)} %param.22) | copy-start | bytes 3440644
  220.6 263.2 %all-gather.6.cloned.1.call-start = ((), (), s32[]{:S(2)}) async-start(), calls=%async_computation.4 | async-start | bytes 9748480 | tf_op jit(solution)/shard_map/all_gather | solution.py:21
Sparse Core Ops, SparseCore 0:
  10.3 101.8 reduce-scatter.7
  115.1 101.0 reduce-scatter.9
  219.0 101.3 reduce-scatter.11
  322.5 53.1 all-gather.7
  378.4 51.3 all-gather.3
  432.4 51.3 all-gather.5
where the time goes:
time: 515 us; the launch traced here: 514 us
  waiting for transfers between devices  366 us (71%)
  local copies, waits for them, and re-layouts  124 us (24%)
  between operations  14.2 us (3%)
  other arithmetic  9.46 us (2%)
    unnamed x8, waiting for transfers between devices  201 us
    all_gather x3, waiting for transfers between devices, step(): whole = [lax.all_gather(one[0], 'dp', axis=1, tiled=True) for one in new]  159 us
    unnamed x19, local copies, waits for them, and re-layouts  124 us
  transfers between devices with their start and end apart: 6, of which 6 were waited for; matrix products, arithmetic and copies ran while one was open for 21% of the time, Pallas kernels for 0%

commit v1 on v0

v1 whole, which is shorter than its diff:
```python
import functools

import jax
import jax.numpy as jnp
from jax import lax
from jax.experimental import pallas as pl
from jax.experimental.pallas import tpu as pltpu
from jax.sharding import PartitionSpec as P

MESH = pl.DeviceIdType.MESH
F32, BF16 = jnp.float32, jnp.bfloat16
N = 16
LAYERS = 2
TILES = 70
AXES = ((8, 4, 2), (4, 2, 8), (2, 8, 4))
SUB = 10
T = TILES // SUB
CHUNKS = LAYERS * SUB
LEAD = 2
RING0 = 2 * LEAD + 2
RING = 4
VM = pltpu.VMEM
ST1, ST2, ST3, AG3, AG2, AG1, ST0, AG0 = range(8)


def add_into(dst, *srcs):
    total = srcs[0][...].astype(F32)
    for one in srcs[1:]:
        total = total + one[...].astype(F32)
    dst[...] = total.astype(BF16)


def kernel(*refs):
    g, w, m, v = (refs[i : i + 3] for i in range(0, 12, 3))
    moments, new_w = refs[12:14]
    wo = [new_w.at[k] for k in range(3)]
    mo, vo = ([moments.at[i, k] for k in range(3)] for i in range(2))
    D, R1, R2, R3, O1, O2, O3, O4, W, s0r, rr, a0r, snd, ld, mv = refs[14:]
    me = lax.axis_index("dp")

    def bit(b):
        return lax.rem(me // b, 2)

    def flip(i, b):
        return i + b - 2 * b * bit(b)

    core = bit(1)
    mate = flip(me, 1)

    def remote(src, dst, send, recv, to):
        return pltpu.make_async_remote_copy(src, dst, send, recv, device_id={"dp": to}, device_id_type=MESH)

    def arrived(ref, sem):
        remote(ref, ref, snd.at[ST0, 0], sem, mate).wait_recv()

    def loaded(ref, sem):
        pltpu.make_async_copy(ref, ref, sem).wait()

    def where(ch):
        return ch // SUB, pl.ds(lax.rem(ch, SUB) * T, T)

    def owner(k, e1, e2, e3, c):
        b1, b2, b3 = AXES[k]
        return e1 * b1 + e2 * b2 + e3 * b3 + c

    def send_raw(ch):
        l, rows = where(ch)
        for k in range(3):
            for p in range(8):
                j = owner(k, p // 4, p // 2 % 2, p % 2, 1 - core)
                remote(g[k].at[l, j, rows], D.at[k, ch, p], snd.at[ST0, k], s0r.at[k, lax.rem(ch, RING0)], mate).start()

    def load_own(which, ch):
        l, rows = where(ch)
        slot = lax.rem(ch, 2)
        for k in range(3):
            b1, b2, b3 = AXES[k]
            m1, m2, m3 = bit(b1), bit(b2), bit(b3)
            if which == 0:
                for q in range(4):
                    j = owner(k, 1 - m1, q // 2, q % 2, core)
                    pltpu.make_async_copy(g[k].at[l, j, rows], O1.at[k, slot, q], ld.at[0, k, slot]).start()
            elif which == 1:
                for q in range(2):
                    j = owner(k, m1, 1 - m2, q, core)
                    pltpu.make_async_copy(g[k].at[l, j, rows], O2.at[k, slot, q], ld.at[1, k, slot]).start()
            elif which == 2:
                j = owner(k, m1, m2, 1 - m3, core)
                pltpu.make_async_copy(g[k].at[l, j, rows], O3.at[k, slot], ld.at[2, k, slot]).start()
            else:
                pltpu.make_async_copy(g[k].at[l, me, rows], O4.at[k, slot], ld.at[3, k, slot]).start()
                pltpu.make_async_copy(w[k].at[l, me, rows], W.at[k, slot], ld.at[4, k, slot]).start()

    def stage1(ch):
        slot = lax.rem(ch, 2)
        for k in range(3):
            b1, b2, b3 = AXES[k]
            base = 4 * (1 - bit(b1))
            arrived(D.at[k, ch], s0r.at[k, lax.rem(ch, RING0)])
            loaded(O1.at[k, slot], ld.at[0, k, slot])

            def one(q, _):
                add_into(D.at[k, ch, base + q], O1.at[k, slot, q], D.at[k, ch, base + q])
                return 0

            lax.fori_loop(0, 4, one, 0)
            remote(D.at[k, ch, pl.ds(base, 4)], R1.at[k, ch], snd.at[ST1, k], rr.at[ST1, k, lax.rem(ch, RING)], flip(me, b1)).start()

    def stage2(ch):
        slot, ring = lax.rem(ch, 2), lax.rem(ch, RING)
        for k in range(3):
            b1, b2, b3 = AXES[k]
            half = 2 * (1 - bit(b2))
            base = 4 * bit(b1) + half
            arrived(R1.at[k, ch], rr.at[ST1, k, ring])
            loaded(O2.at[k, slot], ld.at[1, k, slot])

            def one(q, _):
                add_into(D.at[k, ch, base + q], O2.at[k, slot, q], D.at[k, ch, base + q], R1.at[k, ch, half + q])
                return 0

            lax.fori_loop(0, 2, one, 0)
            remote(D.at[k, ch, pl.ds(base, 2)], R2.at[k, ch], snd.at[ST2, k], rr.at[ST2, k, ring], flip(me, b2)).start()

    def stage3(ch):
        slot, ring = lax.rem(ch, 2), lax.rem(ch, RING)
        for k in range(3):
            b1, b2, b3 = AXES[k]
            m1, m2, n3 = bit(b1), bit(b2), 1 - bit(b3)
            mine = D.at[k, ch, 4 * m1 + 2 * m2 + n3]
            arrived(R2.at[k, ch], rr.at[ST2, k, ring])
            loaded(O3.at[k, slot], ld.at[2, k, slot])
            add_into(mine, O3.at[k, slot], mine, R1.at[k, ch, 2 * m2 + n3], R2.at[k, ch, n3])
            remote(mine, R3.at[k, ch], snd.at[ST3, k], rr.at[ST3, k, ring], flip(me, b3)).start()

    def give(k, ch, stage, blocks, to):
        l, rows = where(ch)
        recv = a0r.at[k] if stage == AG0 else rr.at[stage, k, lax.rem(ch, RING)]
        for j in blocks:
            part = wo[k].at[l, j, rows]
            remote(part, part, snd.at[stage, k], recv, to).start()

    def update(ch):
        l, rows = where(ch)
        slot, ring = lax.rem(ch, 2), lax.rem(ch, RING)
        for k in range(3):
            b1, b2, b3 = AXES[k]
            m1, m2, m3 = bit(b1), bit(b2), bit(b3)
            arrived(R3.at[k, ch], rr.at[ST3, k, ring])
            loaded(O4.at[k, slot], ld.at[3, k, slot])
            loaded(W.at[k, slot], ld.at[4, k, slot])
            total = O4[k, slot].astype(F32)
            for one in (D.at[k, ch, 4 * m1 + 2 * m2 + m3], R1.at[k, ch, 2 * m2 + m3], R2.at[k, ch, m3], R3.at[k, ch]):
                total = total + one[...].astype(F32)
            grad = total.astype(BF16).astype(F32)
            new_m = 0.9 * mo[k][l, rows] + 0.1 * grad
            new_v = 0.95 * vo[k][l, rows] + 0.05 * grad * grad
            old = W[k, slot].astype(F32)
            mo[k][l, rows] = new_m
            vo[k][l, rows] = new_v
            wo[k][l, me, rows] = (old - 0.02 * (new_m * lax.rsqrt(new_v + 1e-8) + 0.1 * old)).astype(BF16)
            give(k, ch, AG3, (me,), flip(me, b3))
            give(k, ch, AG0, (me,), mate)

    def double3(ch):
        l, rows = where(ch)
        for k in range(3):
            b1, b2, b3 = AXES[k]
            got = flip(me, b3)
            arrived(wo[k].at[l, got, rows], rr.at[AG3, k, lax.rem(ch, RING)])
            give(k, ch, AG2, (me, got), flip(me, b2))
            give(k, ch, AG0, (got,), mate)

    def double2(ch):
        l, rows = where(ch)
        for k in range(3):
            b1, b2, b3 = AXES[k]
            held = (me, flip(me, b3))
            got = tuple(flip(j, b2) for j in held)
            arrived(wo[k].at[l, pl.ds(0, 2), rows], rr.at[AG2, k, lax.rem(ch, RING)])
            give(k, ch, AG1, held + got, flip(me, b1))
            give(k, ch, AG0, got, mate)

    def double1(ch):
        l, rows = where(ch)
        for k in range(3):
            b1, b2, b3 = AXES[k]
            held = (me, flip(me, b3))
            got = tuple(flip(j, b1) for j in held + tuple(flip(j, b2) for j in held))
            arrived(wo[k].at[l, pl.ds(0, 4), rows], rr.at[AG1, k, lax.rem(ch, RING)])
            give(k, ch, AG0, got, mate)

    load_own(0, 0)
    for k in range(3):
        pltpu.make_async_copy(m[k], mo[k], mv.at[0, k]).start()
        pltpu.make_async_copy(v[k], vo[k], mv.at[1, k]).start()

    barrier = pltpu.get_barrier_semaphore()
    for b in (1, 2, 4, 8):
        pl.semaphore_signal(barrier, inc=1, device_id={"dp": flip(me, b)}, device_id_type=MESH)
    pl.semaphore_wait(barrier, 4)

    for ch in range(LEAD):
        send_raw(ch)

    for k in range(3):
        loaded(mo[k], mv.at[0, k])
        loaded(vo[k], mv.at[1, k])

    def step(s, _):
        def at(lag, do, *args):
            ch = s - lag

            @pl.when((ch >= 0) & (ch < CHUNKS))
            def _():
                do(*args, ch)

        at(-LEAD, send_raw)
        at(-1, load_own, 0)
        at(0, load_own, 1)
        at(1, load_own, 2)
        at(2, load_own, 3)
        at(0, stage1)
        at(1, stage2)
        at(2, stage3)
        at(3, update)
        at(4, double3)
        at(5, double2)
        at(6, double1)
        return 0

    lax.fori_loop(0, CHUNKS + 6, step, 0)

    for k in range(3):
        arrived(wo[k].at[:, pl.ds(0, 8)], a0r.at[k])
        for stage, sent in (
            (ST0, D.at[k]),
            (ST1, R1.at[k]),
            (ST2, R2.at[k]),
            (ST3, R3.at[k]),
            (AG3, wo[k].at[:, pl.ds(0, 1)]),
            (AG2, wo[k].at[:, pl.ds(0, 2)]),
            (AG1, wo[k].at[:, pl.ds(0, 4)]),
            (AG0, wo[k].at[:, pl.ds(0, 8)]),
        ):
            remote(sent, sent, snd.at[stage, k], a0r.at[k], mate).wait_send()


def write_out(*refs):
    moments, new_w, *targets, sem = refs
    sources = [new_w.at[k] for k in range(3)] + [moments.at[i, k] for i in range(2) for k in range(3)]
    copies = [pltpu.make_async_copy(one, other, sem.at[i]) for i, (one, other) in enumerate(zip(sources, targets, strict=True))]
    for copy in copies:
        copy.start()
    for copy in copies:
        copy.wait()


def tiled(a, parts):
    rows, columns = a.shape[1] // parts // 8, a.shape[2] // 128
    a = a.reshape(LAYERS, parts, rows, 8, columns, 128).transpose(0, 1, 2, 4, 3, 5)
    return a.reshape(LAYERS, parts, TILES, 16, 128)


def untiled(a, shape):
    rows, columns = shape[1] // a.shape[1] // 8, shape[2] // 128
    a = a.reshape(LAYERS, a.shape[1], rows, columns, 8, 128).transpose(0, 1, 2, 4, 3, 5)
    return a.reshape(shape)


def solution(mesh):
    def step(*arrays):
        terms, weights, m, v = (arrays[i : i + 3] for i in (0, 3, 6, 9))
        whole, part = (LAYERS, N, TILES, 16, 128), (LAYERS, TILES, 16, 128)
        block = (T, 16, 128)
        dma = pltpu.SemaphoreType.DMA
        new = pl.pallas_call(
            kernel,
            out_shape=[VM((2, 3, *part), F32), VM((3, *whole), BF16)],
            in_specs=[pl.BlockSpec(memory_space=pltpu.HBM)] * 12,
            out_specs=[pl.BlockSpec(memory_space=pltpu.VMEM)] * 2,
            scratch_shapes=[
                pltpu.VMEM((3, CHUNKS, 8, *block), BF16),
                pltpu.VMEM((3, CHUNKS, 4, *block), BF16),
                pltpu.VMEM((3, CHUNKS, 2, *block), BF16),
                pltpu.VMEM((3, CHUNKS, *block), BF16),
                pltpu.VMEM((3, 2, 4, *block), BF16),
                pltpu.VMEM((3, 2, 2, *block), BF16),
                pltpu.VMEM((3, 2, *block), BF16),
                pltpu.VMEM((3, 2, *block), BF16),
                pltpu.VMEM((3, 2, *block), BF16),
                dma((3, RING0)),
                dma((6, 3, RING)),
                dma((3,)),
                dma((8, 3)),
                dma((5, 3, 2)),
                dma((2, 3)),
            ],
            compiler_params=pltpu.CompilerParams(collective_id=0, has_side_effects=True, vmem_limit_bytes=28 * 2**20),
            name="sum_step_gather",
        )(
            *(tiled(t[0], N) for t in terms),
            *(tiled(one, N) for one in weights),
            *(tiled(one, 1)[:, 0] for one in (*m, *v)),
        )
        new = pl.pallas_call(
            write_out,
            out_shape=[jax.ShapeDtypeStruct(whole, BF16)] * 3 + [jax.ShapeDtypeStruct(part, F32)] * 6,
            in_specs=[pl.BlockSpec(memory_space=pltpu.VMEM)] * 2,
            out_specs=[pl.BlockSpec(memory_space=pltpu.HBM)] * 9,
            scratch_shapes=[dma((9,))],
            compiler_params=pltpu.CompilerParams(vmem_limit_bytes=2**20),
            name="write_out",
        )(*new)
        return (
            *(untiled(one, w.shape) for one, w in zip(new[:3], weights, strict=True)),
            *(untiled(one[:, None], old.shape) for one, old in zip(new[3:], (*m, *v), strict=True)),
        )

    all_of, cut = P(None, None, None), P(None, "dp", None)
    return jax.shard_map(
        step,
        mesh=mesh,
        in_specs=(P(("rep", "dp"), None, None, None),) * 3 + (all_of,) * 3 + (cut,) * 6,
        out_specs=(P("rep", None, None),) * 3 + (P("rep", "dp", None),) * 6,
        check_vma=False,
    )
```

time: 515 us -> 195 us (0.38)
  waiting for transfers between devices: 366 us -> 0 us
  Pallas kernels: 0 us -> 194 us
  local copies, waits for them, and re-layouts: 124 us -> 0 us
  between operations: 14.2 us -> 0.65 us
  other arithmetic: 9.46 us -> 0 us
    unnamed x8 -> x0, waiting for transfers between devices: 201 us -> none
    pallas_call x0 -> x2, Pallas kernels: none -> 194 us  [the longest x1 183 us: step(): pl.pallas_call(kernel, out_shape=[VM((2, 3, *part), F32), VM((3, *whole),...]
    all_gather x3 -> x0, waiting for transfers between devices: 159 us -> none  [step(): whole = [lax.all_gather(one[0], 'dp', axis=1, tiled=True) for one in new]]
    unnamed x19 -> x0, local copies, waits for them, and re-layouts: 124 us -> none
    convert_element_type x3 -> x0, other arithmetic: 9.46 us -> none  [adamw(): return ((w - 0.02 * step).astype(jnp.bfloat16), m, v)]
    reduce_scatter x1 -> x0, waiting for transfers between devices: 6.67 us -> none  [step(): lax.psum_scatter(t[0], 'dp', scatter_dimension=1, tiled=True)]
  transfers between devices with their start and end apart: 6 -> 0, of which waited for: 6 -> 0; matrix products, arithmetic and copies ran while one was open for 21% -> 0% of each run, Pallas kernels for 0% -> 0%
where the time goes in v1:
time: 195 us
  Pallas kernels  194 us (99%)
    pallas_call x1, Pallas kernels, step(): pl.pallas_call(kernel, out_shape=[VM((2, 3, *part), F32), VM((3, *whole),...  183 us
    pallas_call x1, Pallas kernels, step(): pl.pallas_call(write_out, out_shape=[jax.ShapeDtypeStruct(whole, BF16)] *...  11.3 us

profile of v1, /device:TPU:0, one launch (start us, length us, event | category | flops | bytes accessed | tf_op | source)
XLA Modules:
  0.0 194.8 jit_solution(18176080648417574455)
XLA Ops:
  0.6 182.8 %sum_step_gather.1 = (f32[2,3,2,70,16,128]{5,4,3,2,1,0:T(8,128)S(1)}, bf16[3,2,16,70,16,128]{5,4,3,2,1,0:T(8,128)(2,1)S(1)}) custom-call(bf16[2,16,70,16,128]{4,3,2,1,0:T(8,128)(2,1)} %bitcast.105, bf16[2,16,70,16,128]{4,3,2,1,0:T(8,128)(2,1)} %bitcast.106, bf16[2,16,70,16,128]{4,3,2,1,0:T(8,128)(2,1)} %bitcast.107, bf16[2,16,70,16,128]{4,3,2,1,0:T(8,128)(2,1)} %bitcast.108, ...), custom_call_target="tpu_custom_call" | custom-call | tf_op jit(solution)/shard_map/sum_step_gather/pallas_call | solution.py:277
  183.4 11.3 %write_out.1 = (bf16[2,16,70,16,128]{4,3,2,1,0:T(8,128)(2,1)}, bf16[2,16,70,16,128]{4,3,2,1,0:T(8,128)(2,1)}, bf16[2,16,70,16,128]{4,3,2,1,0:T(8,128)(2,1)}, f32...) custom-call(f32[2,3,2,70,16,128]{5,4,3,2,1,0:T(8,128)S(1)} %get-tupl, ...), custom_call_target="tpu_custom_call" | custom-call | tf_op jit(solution)/shard_map/write_out/pallas_call | solution.py:306
